TPU v7x, 32 devices: a whole 2x2x4 slice. The times are simulated.
32 devices in a mesh: dp: 4 (over x, y), tp: 8 (over z, core).
Axes of the slice: x: 2, y: 2, z: 4, core: 2. Of those that a mesh axis runs over, the one named last changes fastest.
Arguments:
- x: bfloat16 [8192, 4096], P(('dp', 'tp')), parts along dimension 0
- w_gate: bfloat16 [4096, 10240], P(None, 'tp')
- w_up: bfloat16 [4096, 10240], P(None, 'tp')
- w_down: bfloat16 [10240, 4096], P('tp')
Outputs:
- output: bfloat16 [8192, 4096], P(('dp', 'tp')), parts along dimension 0
There are 4 independent parts. A program takes and returns all parts, laid end to end along the dimension named above; an argument that names none is the same for every part.
All inputs are finite; a program needn't handle non-finite values.
Results may differ from a plain program's by a relative error of at most 0.016.
Values are sent between devices in bfloat16 or wider.
A program may use at most 2 GiB of HBM per device.

v0:
```python
import jax
import jax.numpy as jnp
from jax import lax
from jax.sharding import PartitionSpec as P


def solution(mesh):
    def step(x, w_gate, w_up, w_down):
        rows = lax.all_gather(x, "tp", axis=0, tiled=True)
        gate = jnp.dot(rows, w_gate, preferred_element_type=jnp.float32)
        up = jnp.dot(rows, w_up, preferred_element_type=jnp.float32)
        hidden = (jax.nn.gelu(gate) * up).astype(jnp.bfloat16)
        term = jnp.dot(hidden, w_down, preferred_element_type=jnp.float32).astype(jnp.bfloat16)
        return lax.psum_scatter(term, "tp", scatter_dimension=0, tiled=True)

    return jax.shard_map(
        step,
        mesh=mesh,
        in_specs=(P(("dp", "tp"), None), P(None, "tp"), P(None, "tp"), P("tp", None)),
        out_specs=P(("dp", "tp"), None),
        check_vma=False,
    )
```

profile of v0, /device:TPU:0, one launch (start us, length us, event | category | flops | bytes accessed | tf_op | source)
XLA Modules:
  0.0 422.5 jit_solution(16732271406345901559)
XLA Ops:
  6.5 0.0 all-gather.2.cloned.1.call-start
  6.5 0.7 all-gather.2.cloned.1.call-update
  7.3 0.0 reduce-scatter.2.cloned.1.call-start
  7.3 155.4 %all-gather.2.cloned.1.call-done = bf16[2048,4096]{1,0:T(8,128)(2,1)} async-done(((bf16[256,4096]{1,0:T(8,128)(2,1)}), bf16[2048,4096]{1,0:T(8,128)(2,1)}) %all-gather.2.cloned.1.call-update) | async-done | bytes 16777232 | tf_op jit(solution)/shard_map/all_gather | solution.py:9
  162.7 0.0 copy-start
  162.7 29.2 %fusion.13 = f32[2048,1280]{1,0:T(8,128)} fusion(bf16[2048,4096]{1,0:T(8,128)(2,1)} %all-gather.2.cloned.1.call-done, bf16[4096,1280]{1,0:T(8,128)(2,1)} %param.5), kind=kOutput, calls=%fused_computation.15 | convolution fusion | flops 21474836480 | bytes 37748736 | tf_op jit(solution)/shard_map/dot_general | solution.py:10
  191.9 0.0 copy-done
  191.9 29.6 %fusion.8.clone.4 = bf16[2048,1280]{1,0:T(8,128)(2,1)S(1)} fusion(f32[2048,1280]{1,0:T(8,128)} %fusion.13, bf16[2048,4096]{1,0:T(8,128)(2,1)S(1)} %copy-done, bf16[4096,1280]{1,0:T(8,128)(2,1)} %param.6), kind=kOutput, calls=%fused_computation.10.clone.clone.clone.1 | convolution fusion | flops 21501050880 | bytes 42991616 | tf_op jit(solution)/shard_map/dot_general | solution.py:11
  221.6 27.2 %convolution_convert_fusion = bf16[2048,4096]{1,0:T(8,128)(2,1)} fusion(bf16[1280,4096]{1,0:T(8,128)(2,1)} %param.7, bf16[2048,1280]{1,0:T(8,128)(2,1)S(1)} %fusion.8.clone.4), kind=kOutput, calls=%fused_computation.1 | convolution fusion | flops 21483225088 | bytes 32505856 | tf_op jit(solution)/shard_map/dot_general | solution.py:13
  248.8 0.0 reduce-scatter.2.cloned.1.call-update
  248.8 166.9 %reduce-scatter.2.cloned.1.call-done = bf16[256,4096]{1,0:T(8,128)(2,1)} async-done(((bf16[2048,4096]{1,0:T(8,128)(2,1)}), bf16[256,4096]{1,0:T(8,128)(2,1)}) %reduce-scatter.2.cloned.1.call-update) | async-done | bytes 2097168 | tf_op jit(solution)/shard_map/reduce_scatter | solution.py:14
Async XLA Ops:
  6.5 156.1 %all-gather.2.cloned.1.call-start = ((), (), s32[]{:S(2)}) async-start(), calls=%async_computation.1 | async-start | bytes 18874368 | tf_op jit(solution)/shard_map/all_gather | solution.py:9
  7.3 408.4 %reduce-scatter.2.cloned.1.call-start = ((), (), s32[]{:S(2)}) async-start(), calls=%async_computation.2 | async-start | bytes 18874368 | tf_op jit(solution)/shard_map/reduce_scatter | solution.py:14
  162.7 29.2 %copy-start = (bf16[2048,4096]{1,0:T(8,128)(2,1)S(1)}, bf16[2048,4096]{1,0:T(8,128)(2,1)}, u32[]{:S(2)}) copy-start(bf16[2048,4096]{1,0:T(8,128)(2,1)} %all-gather.2.cloned.1.call-done) | copy-start | bytes 50331652
Sparse Core Ops, SparseCore 0:
  8.9 153.7 all-gather.1
  248.9 166.7 reduce-scatter.1
where the time goes:
time: 423 us
  waiting for transfers between devices  323 us (76%)
  matrix products  86.1 us (20%)
  between operations  13.4 us (3%)
    reduce_scatter x1, waiting for transfers between devices, step(): return lax.psum_scatter(term, 'tp', scatter_dimension=0, tiled=True)  167 us
    all_gather x1, waiting for transfers between devices, step(): rows = lax.all_gather(x, 'tp', axis=0, tiled=True)  155 us
    dot_general x1, matrix products, step(): up = jnp.dot(rows, w_up, preferred_element_type=jnp.float32)  29.6 us
    dot_general x1, matrix products, step(): gate = jnp.dot(rows, w_gate, preferred_element_type=jnp.float32)  29.2 us
    dot_general x1, matrix products, step(): jnp.dot(hidden, w_down, preferred_element_type=jnp.float32)  27.2 us
  transfers between devices with their start and end apart: 2, of which 2 were waited for; matrix products, arithmetic and copies ran while one was open for 0% of the time, Pallas kernels for 0%

commit v1 on v0

v1 whole, which is shorter than its diff:
```python
import functools

import jax
import jax.numpy as jnp
from jax import lax
from jax.experimental import pallas as pl
from jax.experimental.pallas import tpu as pltpu
from jax.sharding import PartitionSpec as P

MESH = pl.DeviceIdType.MESH
F32, BF16 = jnp.float32, jnp.bfloat16

CHUNKS = 2
PIECES = 8
RING = 8
LAG = 2
UNIT = CHUNKS * PIECES


def kernel(
    x, wg, wu, wd, y, tm, ts, vwg, vwu, vwd, xb, hid,
    own1, sib1, stg1, own2, sib2, stg2, rse, rsi,
    w_sem, x_sem, y_sem, tm_recv, ts_recv, ti_send, te_send, ts_send,
    d1_send, d1_recv, d2_send, d2_recv, rse_send, rse_recv, rsi_send, rsi_recv,
):
    me = lax.axis_index("tp")
    chip, core = me // 2, lax.rem(me, 2)
    is_end = jnp.logical_or(chip == 0, chip == 3)
    sibling = me + 1 - 2 * core
    inward = jnp.where(chip < 2, 2, -2)
    to_in, to_out = me + inward, me - inward
    rows = x.shape[0] // CHUNKS
    width = y.shape[1] // PIECES
    tile = min(256, vwg.shape[1])
    tiles = vwg.shape[1] // tile

    weights = [pltpu.make_async_copy(s, d, w_sem.at[i]) for i, (s, d) in enumerate(((wg, vwg), (wu, vwu), (wd, vwd)))]
    for w in weights:
        w.start()

    barrier = pltpu.get_barrier_semaphore()
    pl.semaphore_signal(barrier, inc=1, device_id={"tp": sibling}, device_id_type=MESH)
    pl.semaphore_signal(barrier, inc=1, device_id={"tp": to_in}, device_id_type=MESH)

    @pl.when(is_end)
    def _():
        pl.semaphore_wait(barrier, 2)

    @pl.when(jnp.logical_not(is_end))
    def _():
        pl.semaphore_signal(barrier, inc=1, device_id={"tp": to_out}, device_id_type=MESH)
        pl.semaphore_wait(barrier, 3)

    def remote(src, dst, send, recv, device):
        return pltpu.make_async_remote_copy(
            src_ref=src, dst_ref=dst, send_sem=send, recv_sem=recv, device_id={"tp": device}, device_id_type=MESH
        )

    def x_rows(j):
        return x.at[pl.ds(pl.multiple_of(j * rows, rows), rows), :]

    def own_to_in(j):
        slot = jnp.where(is_end, 0, CHUNKS) + j
        return remote(x_rows(j), tm.at[slot], ti_send.at[j], tm_recv.at[slot], to_in)

    def own_to_out(j):
        return remote(x_rows(j), tm.at[j], te_send.at[j], tm_recv.at[j], to_out)

    def own_to_sibling(j):
        return remote(x_rows(j), ts.at[j], ts_send.at[j], ts_recv.at[j], sibling)

    def on_to_in(j):
        slot = 2 * CHUNKS + j
        return remote(tm.at[j], tm.at[slot], ti_send.at[CHUNKS + j], tm_recv.at[slot], to_in)

    def on_to_out(a):
        return remote(tm.at[a], tm.at[a], te_send.at[a], tm_recv.at[a], to_out)

    def on_to_sibling(a):
        c = CHUNKS + a
        return remote(tm.at[a], ts.at[c], ts_send.at[c], ts_recv.at[c], sibling)

    def wait_arrival(a):
        on_to_out(a).wait_recv()

    def load(c, mine):
        pltpu.make_async_remote_copy(
            src_ref=ts.at[c], dst_ref=ts.at[c], send_sem=ts_send.at[c], recv_sem=ts_recv.at[c],
            device_id={"tp": sibling}, device_id_type=MESH,
        ).wait_recv()
        first = pltpu.make_async_copy(mine, xb.at[pl.ds(0, rows)], x_sem.at[0])
        second = pltpu.make_async_copy(ts.at[c], xb.at[pl.ds(rows, rows)], x_sem.at[1])
        first.start()
        second.start()
        first.wait()
        second.wait()

    def hidden_tile(c, i):
        columns = pl.ds(pl.multiple_of(i * tile, tile), tile)
        gate = jnp.dot(xb[...], vwg[:, columns], preferred_element_type=F32)
        up = jnp.dot(xb[...], vwu[:, columns], preferred_element_type=F32)
        hid[c, :, columns] = (jax.nn.gelu(gate) * up).astype(BF16)

    def hidden(c):
        @pl.loop(0, tiles)
        def _(i):
            hidden_tile(c, i)

    def to_sibling(stg, sib, send, recv, k):
        s = lax.rem(k, RING)
        return remote(stg.at[s], sib.at[s], send.at[s], recv.at[s], sibling)

    def term(flow, k, c, n):
        own, sib, stg, send, recv = flow
        s = lax.rem(k, RING)

        @pl.when(k >= RING)
        def _():
            to_sibling(stg, sib, send, recv, k).wait_send()

        columns = pl.ds(pl.multiple_of(n * width, width), width)
        both = jnp.dot(hid[c], vwd[:, columns], preferred_element_type=F32)
        stg[s] = both[rows:].astype(BF16)
        own[s] = both[:rows]
        to_sibling(stg, sib, send, recv, k).start()

    def chip_sum(flow, k):
        own, sib, stg, send, recv = flow
        s = lax.rem(k, RING)
        to_sibling(stg, sib, send, recv, k).wait_recv()
        return own[s] + sib[s].astype(F32)

    def drain(flow):
        own, sib, stg, send, recv = flow

        @pl.loop(0, RING)
        def _(k):
            to_sibling(stg, sib, send, recv, k).wait_send()

    flow1 = (own1, sib1, stg1, d1_send, d1_recv)
    flow2 = (own2, sib2, stg2, d2_send, d2_recv)

    def end_sum_in(k):
        return remote(rse.at[k], rse.at[k], rse_send.at[k], rse_recv.at[k], to_in)

    def inner_sum_in(k):
        return remote(rse.at[k], rsi.at[k - UNIT], rse_send.at[k], rsi_recv.at[k - UNIT], to_in)

    def sum_out(k):
        return remote(rsi.at[k], rsi.at[k], rsi_send.at[k], rsi_recv.at[k], to_out)

    def result(k):
        j, n = lax.rem(k, UNIT) // PIECES, lax.rem(k, PIECES)
        place = y.at[pl.ds(pl.multiple_of(j * rows, rows), rows), pl.ds(pl.multiple_of(n * width, width), width)]
        return pltpu.make_async_copy(rsi.at[k], place, y_sem.at[lax.rem(k, UNIT)])

    for j in range(CHUNKS):
        own_to_in(j).start()

        @pl.when(jnp.logical_not(is_end))
        def _(j=j):
            own_to_out(j).start()

        own_to_sibling(j).start()

    weights[0].wait()
    weights[1].wait()

    @pl.loop(0, CHUNKS)
    def _(j):
        load(j, x_rows(j))
        hidden(j)

    weights[2].wait()

    @pl.when(is_end)
    def _():
        @pl.loop(0, 3 * CHUNKS)
        def _(a):
            wait_arrival(a)
            on_to_sibling(a).start()
            c = CHUNKS + a
            load(c, tm.at[a])
            hidden(c)

            @pl.loop(0, PIECES + LAG)
            def _(n):
                k = a * PIECES + n

                @pl.when(n < PIECES)
                def _():
                    term(flow1, k, c, n)

                @pl.when(n >= LAG)
                def _():
                    rse[k - LAG] = chip_sum(flow1, k - LAG).astype(BF16)
                    end_sum_in(k - LAG).start()

        @pl.loop(0, UNIT + LAG)
        def _(k):
            @pl.when(k < UNIT)
            def _():
                term(flow2, k, k // PIECES, lax.rem(k, PIECES))

            @pl.when(k >= LAG)
            def _():
                q = k - LAG
                total = chip_sum(flow2, q)
                sum_out(UNIT + q).wait_recv()
                rsi[UNIT + q] = (total + rsi[UNIT + q].astype(F32)).astype(BF16)
                result(UNIT + q).start()

        @pl.loop(0, 3 * UNIT)
        def _(k):
            end_sum_in(k).wait_send()

        @pl.loop(0, UNIT)
        def _(k):
            result(UNIT + k).wait()

    @pl.when(jnp.logical_not(is_end))
    def _():
        @pl.loop(0, CHUNKS)
        def _(j):
            wait_arrival(j)
            on_to_in(j).start()
            on_to_sibling(j).start()
            wait_arrival(CHUNKS + j)
            on_to_out(CHUNKS + j).start()
            on_to_sibling(CHUNKS + j).start()

            @pl.loop(0, 2)
            def _(u):
                a = u * CHUNKS + j
                load(CHUNKS + a, tm.at[a])
                hidden(CHUNKS + a)

        @pl.loop(2 * CHUNKS, 3 * CHUNKS)
        def _(a):
            wait_arrival(a)
            on_to_out(a).start()
            on_to_sibling(a).start()

            @pl.when(a < 3 * CHUNKS - 1)
            def _():
                load(CHUNKS + a, tm.at[a])
                hidden(CHUNKS + a)

        last = 4 * CHUNKS - 1

        def term1(k):
            term(flow1, k, (2 + k // UNIT) * CHUNKS + lax.rem(k, UNIT) // PIECES, lax.rem(k, PIECES))

        def term2(k):
            term(flow2, k, k // PIECES, lax.rem(k, PIECES))

        term1(0)

        @pl.loop(0, 2 * UNIT + LAG)
        def _(p):
            @pl.when(p < 2 * UNIT)
            def _():
                k = UNIT + p
                total = chip_sum(flow1, p)
                end_sum_in(k).wait_recv()
                rse[k] = (total + rse[k].astype(F32)).astype(BF16)
                inner_sum_in(k).start()

            @pl.when(p < 2 * UNIT - 1)
            def _():
                term1(p + 1)

            @pl.when(p >= LAG)
            def _():
                q = p - LAG
                total = chip_sum(flow2, q)
                sum_out(q).wait_recv()
                total = total + rsi[q].astype(F32)

                @pl.when(q < UNIT)
                def _():
                    end_sum_in(q).wait_recv()
                    rsi[q] = (total + rse[q].astype(F32)).astype(BF16)
                    result(q).start()

                @pl.when(q >= UNIT)
                def _():
                    rsi[q] = total.astype(BF16)
                    sum_out(q).start()

            @pl.when(jnp.logical_and(p >= LAG - 1, p < 2 * UNIT + LAG - 1))
            def _():
                term2(p - LAG + 1)

            @pl.when(p == 2)
            def _():
                load(last, tm.at[3 * CHUNKS - 1])

            @pl.when(jnp.logical_and(p >= 3, p < 3 + tiles))
            def _():
                hidden_tile(last, p - 3)

        @pl.loop(0, 2 * UNIT)
        def _(k):
            inner_sum_in(UNIT + k).wait_send()

        @pl.loop(0, UNIT)
        def _(k):
            sum_out(UNIT + k).wait_send()
            result(k).wait()

        @pl.loop(0, CHUNKS)
        def _(j):
            on_to_in(j).wait_send()
            own_to_out(j).wait_send()

        @pl.loop(CHUNKS, 3 * CHUNKS)
        def _(a):
            on_to_out(a).wait_send()

    drain(flow1)
    drain(flow2)

    @pl.loop(0, CHUNKS)
    def _(j):
        own_to_in(j).wait_send()
        own_to_sibling(j).wait_send()

    @pl.loop(0, 3 * CHUNKS)
    def _(a):
        on_to_sibling(a).wait_send()


def solution(mesh):
    def step(x, w_gate, w_up, w_down):
        n_rows, d = x.shape
        ff = w_gate.shape[1]
        rows, width = n_rows // CHUNKS, d // PIECES
        dma = pltpu.SemaphoreType.DMA
        out, _, _ = pl.pallas_call(
            kernel,
            out_shape=[
                jax.ShapeDtypeStruct((n_rows, d), BF16),
                jax.ShapeDtypeStruct((3 * CHUNKS, rows, d), BF16),
                jax.ShapeDtypeStruct((4 * CHUNKS, rows, d), BF16),
            ],
            in_specs=[pl.BlockSpec(memory_space=pltpu.HBM)] * 4,
            out_specs=[pl.BlockSpec(memory_space=pltpu.HBM)] * 3,
            scratch_shapes=[
                pltpu.VMEM((d, ff), BF16),
                pltpu.VMEM((d, ff), BF16),
                pltpu.VMEM((ff, d), BF16),
                pltpu.VMEM((2 * rows, d), BF16),
                pltpu.VMEM((4 * CHUNKS, 2 * rows, ff), BF16),
                *[
                    pltpu.VMEM((RING, rows, width), F32),
                    pltpu.VMEM((RING, rows, width), BF16),
                    pltpu.VMEM((RING, rows, width), BF16),
                ]
                * 2,
                pltpu.VMEM((3 * UNIT, rows, width), BF16),
                pltpu.VMEM((2 * UNIT, rows, width), BF16),
                dma((3,)),
                dma((2,)),
                dma((UNIT,)),
                dma((3 * CHUNKS,)),
                dma((4 * CHUNKS,)),
                dma((2 * CHUNKS,)),
                dma((3 * CHUNKS,)),
                dma((4 * CHUNKS,)),
                dma((RING,)),
                dma((RING,)),
                dma((RING,)),
                dma((RING,)),
                dma((3 * UNIT,)),
                dma((3 * UNIT,)),
                dma((2 * UNIT,)),
                dma((2 * UNIT,)),
            ],
            compiler_params=pltpu.CompilerParams(
                collective_id=0, has_side_effects=True, vmem_limit_bytes=66_000_000
            ),
            name="mlp_line",
        )(x, w_gate, w_up, w_down)
        return out

    return jax.shard_map(
        step,
        mesh=mesh,
        in_specs=(P(("dp", "tp"), None), P(None, "tp"), P(None, "tp"), P("tp", None)),
        out_specs=P(("dp", "tp"), None),
        check_vma=False,
    )
```

time: 423 us -> 202 us (0.48)
  waiting for transfers between devices: 323 us -> 0 us
  Pallas kernels: 0 us -> 199 us
  matrix products: 86.1 us -> 0 us
  between operations: 13.4 us -> 0.01 us
    pallas_call x0 -> x1, Pallas kernels: none -> 199 us  [step(): pl.pallas_call(kernel, out_shape=[jax.ShapeDtypeStruct((n_rows, d), BF16)...]
    reduce_scatter x1 -> x0, waiting for transfers between devices: 167 us -> none  [step(): return lax.psum_scatter(term, 'tp', scatter_dimension=0, tiled=True)]
    all_gather x1 -> x0, waiting for transfers between devices: 155 us -> none  [step(): rows = lax.all_gather(x, 'tp', axis=0, tiled=True)]
    dot_general x3 -> x0, matrix products: 86.1 us -> none  [the longest x1 29.6 us: step(): up = jnp.dot(rows, w_up, preferred_element_type=jnp.float32)]
  transfers between devices with their start and end apart: 2 -> 0, of which waited for: 2 -> 0; matrix products, arithmetic and copies ran while one was open for 0% -> 0% of each run, Pallas kernels for 0% -> 0%
where the time goes in v1:
time: 202 us
  Pallas kernels  199 us (99%)
  local copies, waits for them, and re-layouts  3.13 us (2%)
    pallas_call x1, Pallas kernels, step(): pl.pallas_call(kernel, out_shape=[jax.ShapeDtypeStruct((n_rows, d), BF16)...  199 us

profile of v1, /device:TPU:0, one launch (start us, length us, event | category | flops | bytes accessed | tf_op | source)
XLA Modules:
  0.0 201.7 jit_solution(3774892459048728145)
XLA Ops:
  0.0 198.6 %mlp_line.1 = (bf16[256,4096]{1,0:T(8,128)(2,1)}, bf16[6,128,4096]{2,1,0:T(8,128)(2,1)}, bf16[8,128,4096]{2,1,0:T(8,128)(2,1)}) custom-call(bf16[256,4096]{1,0:T(8,128)(2,1)} %x.1, bf16[4096,1280]{1,0:T(8,128)(2,1)} %wg.1, bf16[4096,1280]{1,0:T(8,128)(2,1)} %wu.1, bf16[1280,4096]{1,0:T(8,128)(2,1)} %wd.1), custom_call_target="tpu_custom_call" | custom-call | tf_op jit(solution)/shard_map/mlp_line/pallas_call | solution.py:340
  198.6 3.1 %copy.6 = bf16[256,4096]{1,0:T(8,128)(2,1)} copy(bf16[256,4096]{1,0:T(8,128)(2,1)} %get-tuple-element.6) | data formatting | bytes 4194304

commit v2 on v1

v2 whole, which is shorter than its diff:
```python
import functools

import jax
import jax.numpy as jnp
from jax import lax
from jax.experimental import pallas as pl
from jax.experimental.pallas import tpu as pltpu
from jax.sharding import PartitionSpec as P

MESH = pl.DeviceIdType.MESH
F32, BF16 = jnp.float32, jnp.bfloat16

CHUNKS = 2
HALVES = 2
PARTS = CHUNKS * HALVES
PIECES = 8
RING = 8
AHEAD = 2
LAG = 2
HELD_END, HELD_INNER = 4, 2
UNIT = CHUNKS * PIECES
HELD = max(HELD_END, HELD_INNER)
FAR = 3


def kernel(
    x, wg, wu, wd, y, tm, ts, vwg, vwu, vwd, xb, acc, hid,
    own1, sib1, stg1, own2, sib2, stg2, rse, rsi,
    w_sem, x_sem, tm_recv, ts_recv, ti_send, te_send, ts_send,
    d1_send, d1_recv, d2_send, d2_recv, rse_send, rse_recv, rsi_send, rsi_recv,
):
    me = lax.axis_index("tp")
    chip, core = me // 2, lax.rem(me, 2)
    is_end = jnp.logical_or(chip == 0, chip == 3)
    sibling = me + 1 - 2 * core
    inward = jnp.where(chip < 2, 2, -2)
    to_in, to_out = me + inward, me - inward
    rows, half = x.shape[0] // CHUNKS, x.shape[1] // HALVES
    width = y.shape[1] // PIECES
    tile = min(256, vwg.shape[1])
    tiles = vwg.shape[1] // tile

    weights = [pltpu.make_async_copy(s, d, w_sem.at[i]) for i, (s, d) in enumerate(((wg, vwg), (wu, vwu), (wd, vwd)))]
    for w in weights:
        w.start()

    barrier = pltpu.get_barrier_semaphore()
    pl.semaphore_signal(barrier, inc=1, device_id={"tp": sibling}, device_id_type=MESH)
    pl.semaphore_signal(barrier, inc=1, device_id={"tp": to_in}, device_id_type=MESH)

    @pl.when(is_end)
    def _():
        pl.semaphore_wait(barrier, 2)

    @pl.when(jnp.logical_not(is_end))
    def _():
        pl.semaphore_signal(barrier, inc=1, device_id={"tp": to_out}, device_id_type=MESH)
        pl.semaphore_wait(barrier, 3)

    def remote(src, dst, send, recv, device):
        return pltpu.make_async_remote_copy(
            src_ref=src, dst_ref=dst, send_sem=send, recv_sem=recv, device_id={"tp": device}, device_id_type=MESH
        )

    def x_part(b):
        j, h = b // HALVES, lax.rem(b, HALVES)
        return x.at[pl.ds(pl.multiple_of(j * rows, rows), rows), pl.ds(pl.multiple_of(h * half, half), half)]

    def own_to_in(b):
        slot = jnp.where(is_end, 0, PARTS) + b
        return remote(x_part(b), tm.at[slot], ti_send, tm_recv.at[slot], to_in)

    def own_to_out(b):
        return remote(x_part(b), tm.at[b], te_send, tm_recv.at[b], to_out)

    def own_to_sibling(b):
        return remote(x_part(b), ts.at[b], ts_send, ts_recv.at[b], sibling)

    def on_to_in(b):
        slot = 2 * PARTS + b
        return remote(tm.at[b], tm.at[slot], ti_send, tm_recv.at[slot], to_in)

    def on_to_out(a):
        return remote(tm.at[a], tm.at[a], te_send, tm_recv.at[a], to_out)

    def on_to_sibling(a):
        c = PARTS + a
        return remote(tm.at[a], ts.at[c], ts_send, ts_recv.at[c], sibling)

    def wait_arrival(a):
        on_to_out(a).wait_recv()

    def wait_bytes(ref, count, sem):
        whole = ref.at[pl.ds(0, count)]
        pltpu.make_async_copy(whole, whole, sem).wait()

    def load(c, h, mine):
        theirs = ts.at[c * HALVES + h]
        remote(theirs, theirs, ts_send, ts_recv.at[c * HALVES + h], sibling).wait_recv()
        first = pltpu.make_async_copy(mine, xb.at[h, pl.ds(0, rows)], x_sem.at[0])
        second = pltpu.make_async_copy(theirs, xb.at[h, pl.ds(rows, rows)], x_sem.at[1])
        first.start()
        second.start()
        first.wait()
        second.wait()

    def product(weight, columns, h):
        return jnp.dot(xb[h], weight[pl.ds(h * half, half), columns], preferred_element_type=F32)

    def finish(c, columns, gate, up):
        hid[c, :, columns] = (jax.nn.gelu(gate) * up).astype(BF16)

    def hidden_tile(c, i):
        columns = pl.ds(pl.multiple_of(i * tile, tile), tile)
        gate = product(vwg, columns, 0) + product(vwg, columns, 1)
        up = product(vwu, columns, 0) + product(vwu, columns, 1)
        finish(c, columns, gate, up)

    def hidden_first():
        @pl.loop(0, tiles)
        def _(i):
            columns = pl.ds(pl.multiple_of(i * tile, tile), tile)
            acc[0, :, columns] = product(vwg, columns, 0)
            acc[1, :, columns] = product(vwu, columns, 0)

    def hidden_second(c):
        @pl.loop(0, tiles)
        def _(i):
            columns = pl.ds(pl.multiple_of(i * tile, tile), tile)
            gate = acc[0, :, columns] + product(vwg, columns, 1)
            up = acc[1, :, columns] + product(vwu, columns, 1)
            finish(c, columns, gate, up)

    def to_sibling(stg, sib, send, recv, k):
        s = lax.rem(k, RING)
        return remote(stg.at[s], sib.at[s], send.at[s], recv.at[s], sibling)

    def term(flow, k, c, n):
        own, sib, stg, send, recv = flow
        s = lax.rem(k, RING)

        @pl.when(k >= RING)
        def _():
            to_sibling(stg, sib, send, recv, k).wait_send()

        columns = pl.ds(pl.multiple_of(n * width, width), width)
        both = jnp.dot(hid[c], vwd[:, columns], preferred_element_type=F32)
        stg[s] = both[rows:].astype(BF16)
        own[s] = both[:rows]
        to_sibling(stg, sib, send, recv, k).start()

    def chip_sum(flow, k):
        own, sib, stg, send, recv = flow
        s = lax.rem(k, RING)
        to_sibling(stg, sib, send, recv, k).wait_recv()
        return own[s] + sib[s].astype(F32)

    def drain(flow):
        own, sib, stg, send, recv = flow

        @pl.loop(0, RING)
        def _(k):
            to_sibling(stg, sib, send, recv, k).wait_send()

    flow1 = (own1, sib1, stg1, d1_send, d1_recv)
    flow2 = (own2, sib2, stg2, d2_send, d2_recv)

    def end_sum_in(k):
        return remote(rse.at[k], rse.at[k], rse_send, rse_recv.at[k], to_in)

    def inner_sum_in(k):
        return remote(rse.at[k], rsi.at[k - UNIT], rse_send, rsi_recv.at[k - UNIT], to_in)

    def sum_out(k):
        return remote(rsi.at[k], rsi.at[k], rsi_send, rsi_recv.at[k], to_out)

    def result(k, total):
        j, n = lax.rem(k, UNIT) // PIECES, lax.rem(k, PIECES)
        y[pl.ds(pl.multiple_of(j * rows, rows), rows), pl.ds(pl.multiple_of(n * width, width), width)] = total.astype(BF16)

    def order(k, held, units):
        first = UNIT - held
        rest = units * UNIT - held
        return jnp.where(k < first, k, jnp.where(k < rest, k + held, k - rest + first))

    for b in range(PARTS):
        own_to_in(b).start()

        @pl.when(jnp.logical_not(is_end))
        def _(b=b):
            own_to_out(b).start()

        own_to_sibling(b).start()

    weights[0].wait()
    weights[1].wait()

    @pl.loop(0, CHUNKS)
    def _(j):
        for h in range(HALVES):
            load(j, h, x_part(j * HALVES + h))

        @pl.loop(0, tiles)
        def _(i):
            hidden_tile(j, i)

    weights[2].wait()

    def end_pieces(start, stop):
        @pl.loop(start, stop + AHEAD)
        def _(k):
            @pl.when(k < stop)
            def _():
                piece = order(k, HELD_END, 3)
                term(flow1, k, CHUNKS + piece // PIECES, lax.rem(piece, PIECES))

            @pl.when(k >= start + AHEAD)
            def _():
                piece = order(k - AHEAD, HELD_END, 3)
                rse[piece] = chip_sum(flow1, k - AHEAD).astype(BF16)
                end_sum_in(piece).start()

    @pl.when(is_end)
    def _():
        @pl.loop(0, 3 * CHUNKS)
        def _(a):
            c = CHUNKS + a
            for h in range(HALVES):
                part = a * HALVES + h
                wait_arrival(part)
                on_to_sibling(part).start()
                load(c, h, tm.at[part])
                if h == 0:
                    hidden_first()
                else:
                    hidden_second(c)

            start = a * PIECES - jnp.where(a >= CHUNKS, HELD_END, 0)
            stop = (a + 1) * PIECES - jnp.where(a >= CHUNKS - 1, HELD_END, 0)
            end_pieces(start, stop)

        end_pieces(3 * UNIT - HELD_END, 3 * UNIT)

        @pl.loop(0, UNIT + AHEAD)
        def _(k):
            @pl.when(k < UNIT)
            def _():
                term(flow2, k, k // PIECES, lax.rem(k, PIECES))

            @pl.when(k >= AHEAD)
            def _():
                q = k - AHEAD
                total = chip_sum(flow2, q)
                sum_out(UNIT + q).wait_recv()
                result(q, total + rsi[UNIT + q].astype(F32))

        wait_bytes(rse, 3 * UNIT, rse_send)
        wait_bytes(tm, PARTS, ti_send)

    @pl.when(jnp.logical_not(is_end))
    def _():
        def inner_arrivals(j, h):
            b = j * HALVES + h
            wait_arrival(b)
            on_to_in(b).start()
            on_to_sibling(b).start()
            wait_arrival(PARTS + b)
            on_to_out(PARTS + b).start()
            on_to_sibling(PARTS + b).start()

        def far(j, h):
            a = 2 * PARTS + j * HALVES + h
            wait_arrival(a)
            on_to_out(a).start()
            on_to_sibling(a).start()

        def load_arrived(c, h):
            load(c, h, tm.at[(c - CHUNKS) * HALVES + h])

        @pl.loop(0, CHUNKS)
        def _(j):
            inner_arrivals(j, 0)
            load_arrived(CHUNKS + j, 0)
            hidden_first()
            inner_arrivals(j, 1)
            load_arrived(CHUNKS + j, 1)
            hidden_second(CHUNKS + j)
            load_arrived(2 * CHUNKS + j, 0)
            load_arrived(2 * CHUNKS + j, 1)

            @pl.loop(0, tiles)
            def _(i):
                hidden_tile(2 * CHUNKS + j, i)

        far(0, 0)
        load_arrived(3 * CHUNKS, 0)
        hidden_first()
        far(0, 1)
        load_arrived(3 * CHUNKS, 1)
        hidden_second(3 * CHUNKS)
        last = 4 * CHUNKS - 1

        def term1(k):
            piece = order(k, HELD_INNER, 2)
            term(flow1, k, 2 * CHUNKS + piece // PIECES, lax.rem(piece, PIECES))

        def place2(p):
            first, rest = UNIT - HELD, 2 * UNIT - HELD_INNER
            piece = jnp.where(p < first, p, jnp.where(p < rest, p + HELD_INNER, p - rest + first))
            count = jnp.where(p < first, p, p - (HELD - HELD_INNER))
            return piece, count, jnp.logical_or(p < first, p >= UNIT - HELD_INNER)

        stop2 = 2 * UNIT - HELD_INNER + HELD

        def term2(p):
            piece, count, present = place2(p)

            @pl.when(jnp.logical_and(present, jnp.logical_and(p >= 0, p < stop2)))
            def _():
                term(flow2, count, piece // PIECES, lax.rem(piece, PIECES))

        term1(0)

        @pl.loop(0, stop2 + LAG)
        def _(p):
            @pl.when(p < 2 * UNIT)
            def _():
                k = UNIT + order(p, HELD_INNER, 2)
                total = chip_sum(flow1, p)
                end_sum_in(k).wait_recv()
                rse[k] = (total + rse[k].astype(F32)).astype(BF16)
                inner_sum_in(k).start()

            @pl.when(p < 2 * UNIT - 1)
            def _():
                term1(p + 1)

            q, count, present = place2(p - LAG)

            @pl.when(jnp.logical_and(p >= LAG, present))
            def _():
                total = chip_sum(flow2, count)
                sum_out(q).wait_recv()
                total = total + rsi[q].astype(F32)

                @pl.when(q < UNIT)
                def _():
                    end_sum_in(q).wait_recv()
                    result(q, total + rse[q].astype(F32))

                @pl.when(q >= UNIT)
                def _():
                    rsi[q] = total.astype(BF16)
                    sum_out(q).start()

            term2(p - LAG + 1)

            @pl.when(p == FAR)
            def _():
                far(1, 0)
                far(1, 1)

            @pl.when(p == FAR + 2)
            def _():
                load_arrived(last, 0)
                load_arrived(last, 1)

            @pl.when(jnp.logical_and(p >= FAR + 2, p < FAR + 2 + tiles))
            def _():
                hidden_tile(last, p - FAR - 2)

        wait_bytes(rse, 2 * UNIT, rse_send)
        wait_bytes(rsi, UNIT, rsi_send)
        wait_bytes(tm, 2 * PARTS, ti_send)
        wait_bytes(tm, 3 * PARTS, te_send)

    drain(flow1)
    drain(flow2)
    wait_bytes(ts, 4 * PARTS, ts_send)


def solution(mesh):
    def step(x, w_gate, w_up, w_down):
        n_rows, d = x.shape
        ff = w_gate.shape[1]
        rows, width = n_rows // CHUNKS, d // PIECES
        dma = pltpu.SemaphoreType.DMA
        out, _, _ = pl.pallas_call(
            kernel,
            out_shape=[
                pltpu.VMEM((n_rows, d), BF16),
                jax.ShapeDtypeStruct((3 * PARTS, rows, d // HALVES), BF16),
                jax.ShapeDtypeStruct((4 * PARTS, rows, d // HALVES), BF16),
            ],
            in_specs=[pl.BlockSpec(memory_space=pltpu.HBM)] * 4,
            out_specs=[pl.BlockSpec(memory_space=pltpu.VMEM)] + [pl.BlockSpec(memory_space=pltpu.HBM)] * 2,
            scratch_shapes=[
                pltpu.VMEM((d, ff), BF16),
                pltpu.VMEM((d, ff), BF16),
                pltpu.VMEM((ff, d), BF16),
                pltpu.VMEM((HALVES, 2 * rows, d // HALVES), BF16),
                pltpu.VMEM((2, 2 * rows, ff), F32),
                pltpu.VMEM((4 * CHUNKS, 2 * rows, ff), BF16),
                *[
                    pltpu.VMEM((RING, rows, width), F32),
                    pltpu.VMEM((RING, rows, width), BF16),
                    pltpu.VMEM((RING, rows, width), BF16),
                ]
                * 2,
                pltpu.VMEM((3 * UNIT, rows, width), BF16),
                pltpu.VMEM((2 * UNIT, rows, width), BF16),
                dma((3,)),
                dma((2,)),
                dma((3 * PARTS,)),
                dma((4 * PARTS,)),
                dma,
                dma,
                dma,
                dma((RING,)),
                dma((RING,)),
                dma((RING,)),
                dma((RING,)),
                dma,
                dma((3 * UNIT,)),
                dma,
                dma((2 * UNIT,)),
            ],
            compiler_params=pltpu.CompilerParams(
                collective_id=0, has_side_effects=True, vmem_limit_bytes=64_000_000
            ),
            name="mlp_line",
        )(x, w_gate, w_up, w_down)
        return out

    return jax.shard_map(
        step,
        mesh=mesh,
        in_specs=(P(("dp", "tp"), None), P(None, "tp"), P(None, "tp"), P("tp", None)),
        out_specs=P(("dp", "tp"), None),
        check_vma=False,
    )
```

time: 202 us -> 189 us (0.936)
  Pallas kernels: 199 us -> 186 us
    pallas_call x1, Pallas kernels: 199 us -> 186 us  [step(): pl.pallas_call(kernel, out_shape=[pltpu.VMEM((n_rows, d), BF16), jax.Shap...]
where the time goes in v2:
time: 189 us; the launch traced here: 188 us
  Pallas kernels  186 us (98%)
    pallas_call x1, Pallas kernels, step(): pl.pallas_call(kernel, out_shape=[pltpu.VMEM((n_rows, d), BF16), jax.Shap...  186 us

profile of v2, /device:TPU:0, one launch (start us, length us, event | category | flops | bytes accessed | tf_op | source)
XLA Modules:
  0.0 187.8 jit_solution(2618728258435198690)
XLA Ops:
  0.0 186.5 %mlp_line.1 = (bf16[256,4096]{1,0:T(8,128)(2,1)S(1)}, bf16[12,128,2048]{2,1,0:T(8,128)(2,1)}, bf16[16,128,2048]{2,1,0:T(8,128)(2,1)}) custom-call(bf16[256,4096]{1,0:T(8,128)(2,1)} %x.1, bf16[4096,1280]{1,0:T(8,128)(2,1)} %wg.1, bf16[4096,1280]{1,0:T(8,128)(2,1)} %wu.1, bf16[1280,4096]{1,0:T(8,128)(2,1)} %wd.1), custom_call_target="tpu_custom_call" | custom-call | tf_op jit(solution)/shard_map/mlp_line/pallas_call | solution.py:388
  186.5 1.3 copy.6

commit v3 on v2

--- a/solution.py
+++ b/solution.py
@@ -14,12 +14,14 @@
 HALVES = 2
 PARTS = CHUNKS * HALVES
 PIECES = 8
-RING = 8
+RING = 6
 AHEAD = 2
+NEXT = 2
 LAG = 2
 HELD_END, HELD_INNER = 4, 2
 UNIT = CHUNKS * PIECES
 HELD = max(HELD_END, HELD_INNER)
+EARLY = UNIT - HELD
 FAR = 3
 
 
@@ -40,22 +42,19 @@
     tile = min(256, vwg.shape[1])
     tiles = vwg.shape[1] // tile
 
+    barrier = pltpu.get_barrier_semaphore()
+    pl.semaphore_signal(barrier, inc=1, device_id={"tp": sibling}, device_id_type=MESH)
+    pl.semaphore_signal(barrier, inc=1, device_id={"tp": to_in}, device_id_type=MESH)
+
+    @pl.when(jnp.logical_not(is_end))
+    def _():
+        pl.semaphore_signal(barrier, inc=1, device_id={"tp": to_out}, device_id_type=MESH)
+
     weights = [pltpu.make_async_copy(s, d, w_sem.at[i]) for i, (s, d) in enumerate(((wg, vwg), (wu, vwu), (wd, vwd)))]
     for w in weights:
         w.start()
 
-    barrier = pltpu.get_barrier_semaphore()
-    pl.semaphore_signal(barrier, inc=1, device_id={"tp": sibling}, device_id_type=MESH)
-    pl.semaphore_signal(barrier, inc=1, device_id={"tp": to_in}, device_id_type=MESH)
-
-    @pl.when(is_end)
-    def _():
-        pl.semaphore_wait(barrier, 2)
-
-    @pl.when(jnp.logical_not(is_end))
-    def _():
-        pl.semaphore_signal(barrier, inc=1, device_id={"tp": to_out}, device_id_type=MESH)
-        pl.semaphore_wait(barrier, 3)
+    pl.semaphore_wait(barrier, jnp.where(is_end, 2, 3))
 
     def remote(src, dst, send, recv, device):
         return pltpu.make_async_remote_copy(
@@ -74,7 +73,7 @@
         return remote(x_part(b), tm.at[b], te_send, tm_recv.at[b], to_out)
 
     def own_to_sibling(b):
-        return remote(x_part(b), ts.at[b], ts_send, ts_recv.at[b], sibling)
+        return remote(x_part(b), ts.at[b], ts_send, ts_recv.at[0], sibling)
 
     def on_to_in(b):
         slot = 2 * PARTS + b
@@ -84,8 +83,7 @@
         return remote(tm.at[a], tm.at[a], te_send, tm_recv.at[a], to_out)
 
     def on_to_sibling(a):
-        c = PARTS + a
-        return remote(tm.at[a], ts.at[c], ts_send, ts_recv.at[c], sibling)
+        return remote(tm.at[a], ts.at[PARTS + a], ts_send, ts_recv.at[1 + a], sibling)
 
     def wait_arrival(a):
         on_to_out(a).wait_recv()
@@ -96,13 +94,17 @@
 
     def load(c, h, mine):
         theirs = ts.at[c * HALVES + h]
-        remote(theirs, theirs, ts_send, ts_recv.at[c * HALVES + h], sibling).wait_recv()
         first = pltpu.make_async_copy(mine, xb.at[h, pl.ds(0, rows)], x_sem.at[0])
         second = pltpu.make_async_copy(theirs, xb.at[h, pl.ds(rows, rows)], x_sem.at[1])
         first.start()
         second.start()
         first.wait()
         second.wait()
+
+    def load_arrived(c, h):
+        part = (c - CHUNKS) * HALVES + h
+        on_to_sibling(part).wait_recv()
+        load(c, h, tm.at[part])
 
     def product(weight, columns, h):
         return jnp.dot(xb[h], weight[pl.ds(h * half, half), columns], preferred_element_type=F32)
@@ -166,7 +168,7 @@
     flow2 = (own2, sib2, stg2, d2_send, d2_recv)
 
     def end_sum_in(k):
-        return remote(rse.at[k], rse.at[k], rse_send, rse_recv.at[k], to_in)
+        return remote(rse.at[k], rse.at[k], rse_send, rse_recv.at[jnp.maximum(k - EARLY + 1, 0)], to_in)
 
     def inner_sum_in(k):
         return remote(rse.at[k], rsi.at[k - UNIT], rse_send, rsi_recv.at[k - UNIT], to_in)
@@ -194,6 +196,8 @@
 
     weights[0].wait()
     weights[1].wait()
+
+    wait_bytes(ts, PARTS, ts_recv.at[0])
 
     @pl.loop(0, CHUNKS)
     def _(j):
@@ -229,7 +233,7 @@
                 part = a * HALVES + h
                 wait_arrival(part)
                 on_to_sibling(part).start()
-                load(c, h, tm.at[part])
+                load_arrived(c, h)
                 if h == 0:
                     hidden_first()
                 else:
@@ -274,9 +278,6 @@
             on_to_out(a).start()
             on_to_sibling(a).start()
 
-        def load_arrived(c, h):
-            load(c, h, tm.at[(c - CHUNKS) * HALVES + h])
-
         @pl.loop(0, CHUNKS)
         def _(j):
             inner_arrivals(j, 0)
@@ -319,7 +320,11 @@
             def _():
                 term(flow2, count, piece // PIECES, lax.rem(piece, PIECES))
 
-        term1(0)
+        for k in range(NEXT):
+            term1(k)
+
+        for k in range(NEXT - LAG):
+            term2(k)
 
         @pl.loop(0, stop2 + LAG)
         def _(p):
@@ -331,9 +336,9 @@
                 rse[k] = (total + rse[k].astype(F32)).astype(BF16)
                 inner_sum_in(k).start()
 
-            @pl.when(p < 2 * UNIT - 1)
-            def _():
-                term1(p + 1)
+            @pl.when(p < 2 * UNIT - NEXT)
+            def _():
+                term1(p + NEXT)
 
             q, count, present = place2(p - LAG)
 
@@ -343,9 +348,16 @@
                 sum_out(q).wait_recv()
                 total = total + rsi[q].astype(F32)
 
+                @pl.when(q == 0)
+                def _():
+                    wait_bytes(rse, EARLY, rse_recv.at[0])
+
+                @pl.when(jnp.logical_and(q >= EARLY, q < UNIT))
+                def _():
+                    end_sum_in(q).wait_recv()
+
                 @pl.when(q < UNIT)
                 def _():
-                    end_sum_in(q).wait_recv()
                     result(q, total + rse[q].astype(F32))
 
                 @pl.when(q >= UNIT)
@@ -353,7 +365,7 @@
                     rsi[q] = total.astype(BF16)
                     sum_out(q).start()
 
-            term2(p - LAG + 1)
+            term2(p - LAG + NEXT)
 
             @pl.when(p == FAR)
             def _():
@@ -412,7 +424,7 @@
                 dma((3,)),
                 dma((2,)),
                 dma((3 * PARTS,)),
-                dma((4 * PARTS,)),
+                dma((3 * PARTS + 1,)),
                 dma,
                 dma,
                 dma,
@@ -421,7 +433,7 @@
                 dma((RING,)),
                 dma((RING,)),
                 dma,
-                dma((3 * UNIT,)),
+                dma((3 * UNIT - EARLY + 1,)),
                 dma,
                 dma((2 * UNIT,)),
             ],

time: 189 us -> 188 us (level)
  no operation moved by 1% of the time
where the time goes in v3:
time: 188 us
  Pallas kernels  187 us (99%)
    pallas_call x1, Pallas kernels, step(): pl.pallas_call(kernel, out_shape=[pltpu.VMEM((n_rows, d), BF16), jax.Shap...  187 us

profile of v3, /device:TPU:0, one launch (start us, length us, event | category | flops | bytes accessed | tf_op | source)
XLA Modules:
  0.0 187.9 jit_solution(997312784352670563)
XLA Ops:
  0.0 186.5 %mlp_line.1 = (bf16[256,4096]{1,0:T(8,128)(2,1)S(1)}, bf16[12,128,2048]{2,1,0:T(8,128)(2,1)}, bf16[16,128,2048]{2,1,0:T(8,128)(2,1)}) custom-call(bf16[256,4096]{1,0:T(8,128)(2,1)} %x.1, bf16[4096,1280]{1,0:T(8,128)(2,1)} %wg.1, bf16[4096,1280]{1,0:T(8,128)(2,1)} %wu.1, bf16[1280,4096]{1,0:T(8,128)(2,1)} %wd.1), custom_call_target="tpu_custom_call" | custom-call | tf_op jit(solution)/shard_map/mlp_line/pallas_call | solution.py:400
  186.5 1.3 copy.6

commit v4 on v3

--- a/solution.py
+++ b/solution.py
@@ -28,7 +28,7 @@
 def kernel(
     x, wg, wu, wd, y, tm, ts, vwg, vwu, vwd, xb, acc, hid,
     own1, sib1, stg1, own2, sib2, stg2, rse, rsi,
-    w_sem, x_sem, tm_recv, ts_recv, ti_send, te_send, ts_send,
+    ready, w_sem, x_sem, tm_recv, ts_recv, ti_send, te_send, ts_send,
     d1_send, d1_recv, d2_send, d2_recv, rse_send, rse_recv, rsi_send, rsi_recv,
 ):
     me = lax.axis_index("tp")
@@ -43,12 +43,19 @@
     tiles = vwg.shape[1] // tile
 
     barrier = pltpu.get_barrier_semaphore()
-    pl.semaphore_signal(barrier, inc=1, device_id={"tp": sibling}, device_id_type=MESH)
-    pl.semaphore_signal(barrier, inc=1, device_id={"tp": to_in}, device_id_type=MESH)
+    def signal(semaphore, device):
+        pl.semaphore_signal(semaphore, inc=1, device_id={"tp": device}, device_id_type=MESH)
+
+    signal(barrier, sibling)
+
+    @pl.when(is_end)
+    def _():
+        signal(barrier, to_in - core)
 
     @pl.when(jnp.logical_not(is_end))
     def _():
-        pl.semaphore_signal(barrier, inc=1, device_id={"tp": to_out}, device_id_type=MESH)
+        signal(barrier, to_out)
+        signal(barrier, to_in - core + 1)
 
     weights = [pltpu.make_async_copy(s, d, w_sem.at[i]) for i, (s, d) in enumerate(((wg, vwg), (wu, vwu), (wd, vwd)))]
     for w in weights:
@@ -185,14 +192,37 @@
         rest = units * UNIT - held
         return jnp.where(k < first, k, jnp.where(k < rest, k + held, k - rest + first))
 
-    for b in range(PARTS):
-        own_to_in(b).start()
-
-        @pl.when(jnp.logical_not(is_end))
-        def _(b=b):
-            own_to_out(b).start()
-
-        own_to_sibling(b).start()
+    def all_parts(copy):
+        for b in range(PARTS):
+            copy(b).start()
+
+    is_inner = jnp.logical_not(is_end)
+
+    @pl.when(jnp.logical_or(is_end, core == 1))
+    def _():
+        all_parts(own_to_in)
+
+    @pl.when(jnp.logical_and(is_inner, core == 0))
+    def _():
+        all_parts(own_to_out)
+
+    @pl.when(is_inner)
+    def _():
+        signal(ready, sibling)
+
+    all_parts(own_to_sibling)
+
+    @pl.when(is_inner)
+    def _():
+        pl.semaphore_wait(ready, 1)
+
+    @pl.when(jnp.logical_and(is_inner, core == 0))
+    def _():
+        all_parts(own_to_in)
+
+    @pl.when(jnp.logical_and(is_inner, core == 1))
+    def _():
+        all_parts(own_to_out)
 
     weights[0].wait()
     weights[1].wait()
@@ -421,6 +451,7 @@
                 * 2,
                 pltpu.VMEM((3 * UNIT, rows, width), BF16),
                 pltpu.VMEM((2 * UNIT, rows, width), BF16),
+                pltpu.SemaphoreType.REGULAR,
                 dma((3,)),
                 dma((2,)),
                 dma((3 * PARTS,)),

time: 188 us -> 188 us (level)
  no operation moved by 1% of the time
where the time goes in v4:
time: 188 us
  Pallas kernels  187 us (99%)
    pallas_call x1, Pallas kernels, step(): pl.pallas_call(kernel, out_shape=[pltpu.VMEM((n_rows, d), BF16), jax.Shap...  187 us

profile of v4, /device:TPU:0, one launch (start us, length us, event | category | flops | bytes accessed | tf_op | source)
XLA Modules:
  0.0 188.0 jit_solution(12946044861520254931)
XLA Ops:
  0.0 186.7 %mlp_line.1 = (bf16[256,4096]{1,0:T(8,128)(2,1)S(1)}, bf16[12,128,2048]{2,1,0:T(8,128)(2,1)}, bf16[16,128,2048]{2,1,0:T(8,128)(2,1)}) custom-call(bf16[256,4096]{1,0:T(8,128)(2,1)} %x.1, bf16[4096,1280]{1,0:T(8,128)(2,1)} %wg.1, bf16[4096,1280]{1,0:T(8,128)(2,1)} %wu.1, bf16[1280,4096]{1,0:T(8,128)(2,1)} %wd.1), custom_call_target="tpu_custom_call" | custom-call | tf_op jit(solution)/shard_map/mlp_line/pallas_call | solution.py:430
  186.7 1.3 copy.6

commit v5 on v4

--- a/solution.py
+++ b/solution.py
@@ -14,8 +14,8 @@
 HALVES = 2
 PARTS = CHUNKS * HALVES
 PIECES = 8
-RING = 6
-AHEAD = 2
+RING = 4
+AHEAD = 1
 NEXT = 2
 LAG = 2
 HELD_END, HELD_INNER = 4, 2
@@ -28,7 +28,7 @@
 def kernel(
     x, wg, wu, wd, y, tm, ts, vwg, vwu, vwd, xb, acc, hid,
     own1, sib1, stg1, own2, sib2, stg2, rse, rsi,
-    ready, w_sem, x_sem, tm_recv, ts_recv, ti_send, te_send, ts_send,
+    ready, free, w_sem, x_sem, tm_recv, ts_recv, ti_send, te_send, ts_send,
     d1_send, d1_recv, d2_send, d2_recv, rse_send, rse_recv, rsi_send, rsi_recv,
 ):
     me = lax.axis_index("tp")
@@ -99,19 +99,27 @@
         whole = ref.at[pl.ds(0, count)]
         pltpu.make_async_copy(whole, whole, sem).wait()
 
-    def load(c, h, mine):
+    def loads(c, h, mine):
         theirs = ts.at[c * HALVES + h]
-        first = pltpu.make_async_copy(mine, xb.at[h, pl.ds(0, rows)], x_sem.at[0])
-        second = pltpu.make_async_copy(theirs, xb.at[h, pl.ds(rows, rows)], x_sem.at[1])
-        first.start()
-        second.start()
-        first.wait()
-        second.wait()
+        return (
+            pltpu.make_async_copy(mine, xb.at[h, pl.ds(0, rows)], x_sem.at[2 * h]),
+            pltpu.make_async_copy(theirs, xb.at[h, pl.ds(rows, rows)], x_sem.at[2 * h + 1]),
+        )
+
+    def load_start(c, h):
+        part = (c - CHUNKS) * HALVES + h
+        ours, other = loads(c, h, tm.at[part])
+        ours.start()
+        on_to_sibling(part).wait_recv()
+        other.start()
+
+    def load_wait(c, h):
+        for copy in loads(c, h, tm.at[0]):
+            copy.wait()
 
     def load_arrived(c, h):
-        part = (c - CHUNKS) * HALVES + h
-        on_to_sibling(part).wait_recv()
-        load(c, h, tm.at[part])
+        load_start(c, h)
+        load_wait(c, h)
 
     def product(weight, columns, h):
         return jnp.dot(xb[h], weight[pl.ds(h * half, half), columns], preferred_element_type=F32)
@@ -232,7 +240,11 @@
     @pl.loop(0, CHUNKS)
     def _(j):
         for h in range(HALVES):
-            load(j, h, x_part(j * HALVES + h))
+            for copy in loads(j, h, x_part(j * HALVES + h)):
+                copy.start()
+
+        for h in range(HALVES):
+            load_wait(j, h)
 
         @pl.loop(0, tiles)
         def _(i):
@@ -254,20 +266,35 @@
                 rse[piece] = chip_sum(flow1, k - AHEAD).astype(BF16)
                 end_sum_in(piece).start()
 
+    def straight_to_sibling(a, h):
+        return remote(tm.at[a], xb.at[h, pl.ds(rows, rows)], ts_send, ts_recv.at[1 + a], sibling)
+
     @pl.when(is_end)
     def _():
+        for h in range(HALVES):
+            pl.semaphore_signal(free.at[h], inc=1, device_id={"tp": sibling}, device_id_type=MESH)
+
         @pl.loop(0, 3 * CHUNKS)
         def _(a):
             c = CHUNKS + a
             for h in range(HALVES):
                 part = a * HALVES + h
                 wait_arrival(part)
-                on_to_sibling(part).start()
-                load_arrived(c, h)
+                ours = pltpu.make_async_copy(tm.at[part], xb.at[h, pl.ds(0, rows)], x_sem.at[2 * h])
+                ours.start()
+                pl.semaphore_wait(free.at[h], 1)
+                straight = straight_to_sibling(part, h)
+                straight.start()
+                ours.wait()
+                straight.wait_recv()
                 if h == 0:
                     hidden_first()
                 else:
                     hidden_second(c)
+
+                @pl.when(a < 3 * CHUNKS - 1)
+                def _(h=h):
+                    pl.semaphore_signal(free.at[h], inc=1, device_id={"tp": sibling}, device_id_type=MESH)
 
             start = a * PIECES - jnp.where(a >= CHUNKS, HELD_END, 0)
             stop = (a + 1) * PIECES - jnp.where(a >= CHUNKS - 1, HELD_END, 0)
@@ -316,8 +343,10 @@
             inner_arrivals(j, 1)
             load_arrived(CHUNKS + j, 1)
             hidden_second(CHUNKS + j)
-            load_arrived(2 * CHUNKS + j, 0)
-            load_arrived(2 * CHUNKS + j, 1)
+            load_start(2 * CHUNKS + j, 0)
+            load_start(2 * CHUNKS + j, 1)
+            load_wait(2 * CHUNKS + j, 0)
+            load_wait(2 * CHUNKS + j, 1)
 
             @pl.loop(0, tiles)
             def _(i):
@@ -404,12 +433,17 @@
 
             @pl.when(p == FAR + 2)
             def _():
-                load_arrived(last, 0)
-                load_arrived(last, 1)
-
-            @pl.when(jnp.logical_and(p >= FAR + 2, p < FAR + 2 + tiles))
-            def _():
-                hidden_tile(last, p - FAR - 2)
+                load_start(last, 0)
+                load_start(last, 1)
+
+            @pl.when(p == FAR + 3)
+            def _():
+                load_wait(last, 0)
+                load_wait(last, 1)
+
+            @pl.when(jnp.logical_and(p >= FAR + 3, p < FAR + 3 + tiles))
+            def _():
+                hidden_tile(last, p - FAR - 3)
 
         wait_bytes(rse, 2 * UNIT, rse_send)
         wait_bytes(rsi, UNIT, rsi_send)
@@ -452,8 +486,9 @@
                 pltpu.VMEM((3 * UNIT, rows, width), BF16),
                 pltpu.VMEM((2 * UNIT, rows, width), BF16),
                 pltpu.SemaphoreType.REGULAR,
+                pltpu.SemaphoreType.REGULAR((HALVES,)),
                 dma((3,)),
-                dma((2,)),
+                dma((2 * HALVES,)),
                 dma((3 * PARTS,)),
                 dma((3 * PARTS + 1,)),
                 dma,

time: 188 us -> 188 us (level)
  no operation moved by 1% of the time
where the time goes in v5:
time: 188 us; the launch traced here: 187 us
  Pallas kernels  186 us (99%)
    pallas_call x1, Pallas kernels, step(): pl.pallas_call(kernel, out_shape=[pltpu.VMEM((n_rows, d), BF16), jax.Shap...  186 us

profile of v5, /device:TPU:0, one launch (start us, length us, event | category | flops | bytes accessed | tf_op | source)
XLA Modules:
  0.0 186.9 jit_solution(16332657970244731427)
XLA Ops:
  0.0 185.6 %mlp_line.1 = (bf16[256,4096]{1,0:T(8,128)(2,1)S(1)}, bf16[12,128,2048]{2,1,0:T(8,128)(2,1)}, bf16[16,128,2048]{2,1,0:T(8,128)(2,1)}) custom-call(bf16[256,4096]{1,0:T(8,128)(2,1)} %x.1, bf16[4096,1280]{1,0:T(8,128)(2,1)} %wg.1, bf16[4096,1280]{1,0:T(8,128)(2,1)} %wu.1, bf16[1280,4096]{1,0:T(8,128)(2,1)} %wd.1), custom_call_target="tpu_custom_call" | custom-call | tf_op jit(solution)/shard_map/mlp_line/pallas_call | solution.py:464
  185.6 1.3 copy.6

commit v6 on v5

--- a/solution.py
+++ b/solution.py
@@ -50,12 +50,12 @@
 
     @pl.when(is_end)
     def _():
+        signal(barrier, to_in - core + 1)
+
+    @pl.when(jnp.logical_not(is_end))
+    def _():
+        signal(barrier, to_out)
         signal(barrier, to_in - core)
-
-    @pl.when(jnp.logical_not(is_end))
-    def _():
-        signal(barrier, to_out)
-        signal(barrier, to_in - core + 1)
 
     weights = [pltpu.make_async_copy(s, d, w_sem.at[i]) for i, (s, d) in enumerate(((wg, vwg), (wu, vwu), (wd, vwd)))]
     for w in weights:
@@ -206,29 +206,29 @@
 
     is_inner = jnp.logical_not(is_end)
 
-    @pl.when(jnp.logical_or(is_end, core == 1))
+    @pl.when(jnp.logical_or(is_end, core == 0))
     def _():
         all_parts(own_to_in)
 
+    @pl.when(jnp.logical_and(is_inner, core == 1))
+    def _():
+        all_parts(own_to_out)
+
+    @pl.when(is_inner)
+    def _():
+        signal(ready, sibling)
+
+    all_parts(own_to_sibling)
+
+    @pl.when(is_inner)
+    def _():
+        pl.semaphore_wait(ready, 1)
+
+    @pl.when(jnp.logical_and(is_inner, core == 1))
+    def _():
+        all_parts(own_to_in)
+
     @pl.when(jnp.logical_and(is_inner, core == 0))
-    def _():
-        all_parts(own_to_out)
-
-    @pl.when(is_inner)
-    def _():
-        signal(ready, sibling)
-
-    all_parts(own_to_sibling)
-
-    @pl.when(is_inner)
-    def _():
-        pl.semaphore_wait(ready, 1)
-
-    @pl.when(jnp.logical_and(is_inner, core == 0))
-    def _():
-        all_parts(own_to_in)
-
-    @pl.when(jnp.logical_and(is_inner, core == 1))
     def _():
         all_parts(own_to_out)
 

time: 188 us -> 188 us (level)
  no operation moved by 1% of the time
where the time goes in v6:
time: 188 us; the launch traced here: 187 us
  Pallas kernels  186 us (99%)
    pallas_call x1, Pallas kernels, step(): pl.pallas_call(kernel, out_shape=[pltpu.VMEM((n_rows, d), BF16), jax.Shap...  186 us

profile of v6, /device:TPU:0, one launch (start us, length us, event | category | flops | bytes accessed | tf_op | source)
XLA Modules:
  0.0 186.8 jit_solution(1940736579860288543)
XLA Ops:
  0.0 185.5 %mlp_line.1 = (bf16[256,4096]{1,0:T(8,128)(2,1)S(1)}, bf16[12,128,2048]{2,1,0:T(8,128)(2,1)}, bf16[16,128,2048]{2,1,0:T(8,128)(2,1)}) custom-call(bf16[256,4096]{1,0:T(8,128)(2,1)} %x.1, bf16[4096,1280]{1,0:T(8,128)(2,1)} %wg.1, bf16[4096,1280]{1,0:T(8,128)(2,1)} %wu.1, bf16[1280,4096]{1,0:T(8,128)(2,1)} %wd.1), custom_call_target="tpu_custom_call" | custom-call | tf_op jit(solution)/shard_map/mlp_line/pallas_call | solution.py:464
  185.5 1.3 copy.6
